TPU v7x, 32 devices: a whole 2x2x4 slice. The times are simulated.
32 devices in a mesh: sp: 4 (over x, core), tp: 8 (over z, y).
Axes of the slice: x: 2, y: 2, z: 4, core: 2. Of those that a mesh axis runs over, the one named last changes fastest.
Arguments:
- tokens: bfloat16 [8, 220, 4096], P(None, 'sp'), may hold values from -6 to 6
- modulation: float32 [6, 4096], replicated, may hold values from -2.5 to 2.5
- w_qkv: bfloat16 [4096, 3, 4096], P('sp', None, 'tp'), may hold values from -4 to 4
- w_out: bfloat16 [4096, 4096], P('tp', 'sp'), may hold values from -0.09375 to 0.09375
- w_up: bfloat16 [4096, 16384], P('sp', 'tp'), may hold values from -0.09375 to 0.09375
- w_down: bfloat16 [16384, 4096], P('tp', 'sp'), may hold values from -0.046875 to 0.046875
Outputs:
- block_out: bfloat16 [8, 220, 4096], P(None, 'sp', 'tp')
All inputs are finite; a program needn't handle non-finite values.
Results may differ from a plain program's by a relative error of at most 0.012.
Values may be sent and summed in bfloat16 or wider, within the bound.
A program may use at most 128 MiB of HBM per device.

v0:
```python
import math

import jax
import jax.numpy as jnp
from jax import lax
from jax.sharding import PartitionSpec as P

DH = 128
EPSILON = 1e-06
MLP_CHUNKS = 4
BF = jnp.bfloat16
F32 = jnp.float32


def normalize(tok_rows, shift_vec, scale_vec):
    values = tok_rows.astype(F32)
    center = jnp.mean(values, axis=-1, keepdims=True)
    spread = jnp.mean(jnp.square(values - center), axis=-1, keepdims=True)
    scaled = (values - center) * lax.rsqrt(spread + EPSILON)
    return (scaled * (1.0 + scale_vec) + shift_vec).astype(BF)


def reduce_scatter_sp(parts):
    sp_count, n, c = parts.shape
    chips = sp_count // 2
    me = lax.axis_index("sp")
    core, chip = me % 2, me // 2
    pairs = parts.reshape(chips, 2, n, c)
    away = lax.dynamic_index_in_dim(pairs, 1 - core, 1, keepdims=False)
    got = lax.ppermute(away, "sp", [(i, i ^ 1) for i in range(sp_count)])
    mine = lax.dynamic_index_in_dim(pairs, core, 1, keepdims=False)
    both = (mine.astype(F32) + got.astype(F32)).astype(BF)
    total = lax.dynamic_index_in_dim(both, chip, 0, keepdims=False).astype(F32)
    for k in range(1, chips):
        piece = lax.dynamic_index_in_dim(both, (chip + k) % chips, 0, keepdims=False)
        perm = [(i, ((i // 2 + k) % chips) * 2 + i % 2) for i in range(sp_count)]
        total = total + lax.ppermute(piece, "sp", perm).astype(F32)
    return total


def all_gather_sp(piece):
    n, c = piece.shape
    sp_count = lax.axis_size("sp")
    chips = sp_count // 2
    me = lax.axis_index("sp")
    core, chip = me % 2, me // 2
    out = jnp.zeros((chips, 2, n, c), piece.dtype)
    for k in range(chips):
        got = piece
        if k:
            perm = [(i, ((i // 2 + k) % chips) * 2 + i % 2) for i in range(sp_count)]
            got = lax.ppermute(piece, "sp", perm)
        other = lax.ppermute(got, "sp", [(i, i ^ 1) for i in range(sp_count)])
        at = (chip - k) % chips
        out = lax.dynamic_update_slice(out, got[None, None], (at, core, 0, 0))
        out = lax.dynamic_update_slice(out, other[None, None], (at, 1 - core, 0, 0))
    return out.reshape(sp_count, n, c)


def attend(queries, key_rows, values, key_ok):
    factor = queries.shape[-1] ** (-0.5)
    scores = jnp.einsum("iqe,ike->iqk", queries, key_rows, preferred_element_type=F32) * factor
    scores = jnp.where(key_ok, scores, -jnp.inf)
    raw = jnp.exp(scores - jnp.max(scores, axis=-1, keepdims=True))
    att_weights = (raw / jnp.sum(raw, axis=-1, keepdims=True)).astype(BF)
    return jnp.einsum("iqk,ike->iqe", att_weights, values, preferred_element_type=F32).astype(BF)


def shards(tokens, modulation, w_qkv, w_out, w_up, w_down):
    frames, patches, width = tokens.shape
    sp_count, tp_count = lax.axis_size("sp"), lax.axis_size("tp")
    sp_me, tp_me = lax.axis_index("sp"), lax.axis_index("tp")
    heads = w_qkv.shape[2] // DH
    slab = width // sp_count
    groups = math.gcd(frames, tp_count)
    sub, f_own = tp_count // groups, frames // groups
    unit = 8 * sub
    padded = -(-patches // unit) * unit
    part = padded // sub
    rows = sub * sp_count * part
    own_rows = f_own * sp_count * part

    padded_tokens = jnp.pad(tokens, ((0, 0), (0, padded - patches), (0, 0)))
    mine = lax.dynamic_slice(
        padded_tokens, ((tp_me // sub) * f_own, (tp_me % sub) * part, 0), (f_own, part, width)
    )
    mod_mine = normalize(mine, modulation[0], modulation[1])
    def to_slabs(value):
        value = value.reshape(f_own * part, sp_count, slab)
        value = exchange(jnp.transpose(value, (1, 0, 2)), "sp")
        value = value.reshape(sp_count, f_own, part, slab)
        return jnp.transpose(value, (1, 0, 2, 3)).reshape(own_rows, slab)

    mod_slab, tok_slab = to_slabs(mod_mine), to_slabs(mine)
    mod_a = spread_rows(mod_slab, frames, sub, f_own, rows)

    at = jnp.arange(rows)
    key_ok = ((at // (sp_count * part)) * part + at % part) < patches

    chunks = 2 if frames % (2 * sp_count) == 0 else 1
    f_chunk = frames // chunks
    f_split = math.gcd(f_chunk, sp_count)
    h_split = sp_count // f_split
    f_mine, h_mine = f_chunk // f_split, heads // h_split
    w_flat = w_qkv.reshape(slab, 3 * heads * DH)
    attn_parts = []
    for c in range(chunks):
        lhs = mod_a[c * f_chunk : (c + 1) * f_chunk].reshape(f_chunk * rows, slab)
        proj = jnp.dot(lhs, w_flat, preferred_element_type=F32).astype(BF)
        if h_split > 1:
            proj = proj.reshape(f_split, f_mine * rows, 3, h_split, h_mine * DH)
            proj = jnp.transpose(proj, (0, 3, 1, 2, 4))
        proj = proj.reshape(sp_count, f_mine * rows, 3 * h_mine * DH)
        proj = reduce_scatter_sp(proj).astype(BF).reshape(f_mine, rows, 3, h_mine, DH)
        proj = jnp.transpose(proj, (2, 0, 3, 1, 4)).reshape(3, f_mine * h_mine, rows, DH)
        att = attend(proj[0], proj[1], proj[2], key_ok)
        att = jnp.transpose(att.reshape(f_mine, h_mine, rows, DH), (0, 2, 1, 3))
        att = all_gather_sp(att.reshape(f_mine * rows, h_mine * DH))
        if h_split > 1:
            att = att.reshape(f_split, h_split, f_mine * rows, h_mine * DH)
            att = jnp.transpose(att, (0, 2, 1, 3))
        att = att.reshape(f_chunk * rows, heads * DH)
        attn_parts.append(jnp.dot(att, w_out, preferred_element_type=F32).astype(BF))
    attn_part = jnp.concatenate(attn_parts, 0).reshape(tp_count, own_rows, slab)
    attn_sum = reduce_scatter_tp(attn_part)

    mod_slice = lax.dynamic_slice_in_dim(modulation, sp_me * slab, slab, 1)
    middle = (tok_slab.astype(F32) + mod_slice[2] * attn_sum).astype(BF)

    values = middle.astype(F32)
    mean_s = jnp.mean(values, axis=-1)
    dev_s = jnp.sum(jnp.square(values - mean_s[:, None]), axis=-1)
    stats = lax.all_gather(jnp.stack([mean_s, dev_s]), "sp", axis=0)
    center = jnp.mean(stats[:, 0], axis=0)
    spread = (jnp.sum(stats[:, 1], 0) + slab * jnp.sum(jnp.square(stats[:, 0] - center), 0)) / width
    scaled = (values - center[:, None]) * lax.rsqrt(spread + EPSILON)[:, None]
    mod_b = (scaled * (1.0 + mod_slice[4]) + mod_slice[3]).astype(BF)
    mod_b = spread_rows(mod_b, frames, sub, f_own, rows).reshape(frames * rows, slab)

    hid = w_up.shape[1] // MLP_CHUNKS
    share = frames * rows // sp_count
    acc = None
    for c in range(MLP_CHUNKS):
        up = jnp.dot(mod_b, w_up[:, c * hid : (c + 1) * hid], preferred_element_type=F32)
        up = reduce_scatter_sp(up.astype(BF).reshape(sp_count, share, hid))
        hidden = jax.nn.gelu(up, approximate=True).astype(BF)
        hidden = all_gather_sp(hidden).reshape(frames * rows, hid)
        term = jnp.dot(hidden, w_down[c * hid : (c + 1) * hid], preferred_element_type=F32)
        acc = term if acc is None else acc + term
    mlp_part = acc.astype(BF).reshape(tp_count, own_rows, slab)
    mlp_sum = reduce_scatter_tp(mlp_part)
    block = (middle.astype(F32) + mod_slice[5] * mlp_sum).astype(BF)

    block = jnp.transpose(block.reshape(f_own, sp_count, part, slab), (1, 0, 2, 3))
    block = exchange(block.reshape(sp_count, f_own * part, slab), "sp")
    block = jnp.transpose(block, (1, 0, 2)).reshape(f_own * part, tp_count, width // tp_count)
    block = exchange(jnp.transpose(block, (1, 0, 2)), "tp")
    block = block.reshape(groups, sub, f_own, part, width // tp_count)
    block = jnp.transpose(block, (0, 2, 1, 3, 4)).reshape(frames, padded, width // tp_count)
    return block[:, :patches]


def tp_grid():
    count = lax.axis_size("tp")
    lanes = 2 ** ((count.bit_length() - 1) // 2)
    return count, count // lanes, lanes


def ring_shift(value, k):
    count, ring, lanes = tp_grid()
    return lax.ppermute(
        value, "tp", [(i, ((i // lanes + k) % ring) * lanes + i % lanes) for i in range(count)]
    )


def lane_shift(value, k):
    count, ring, lanes = tp_grid()
    return lax.ppermute(
        value, "tp", [(i, (i // lanes) * lanes + (i + k) % lanes) for i in range(count)]
    )


def ring_pieces(piece):
    ring = tp_grid()[1]
    if ring != 4:
        return [(k, ring_shift(piece, k) if k else piece) for k in range(ring)]
    half = piece.shape[1] // 2
    left, right = ring_shift(piece, 1), ring_shift(piece, -1)
    far = [ring_shift(left[:, :half], 1), ring_shift(right[:, half:], -1)]
    return [(0, piece), (1, left), (3, right), (2, jnp.concatenate(far, 1))]


def ring_reduce(parts):
    ring = parts.shape[0]
    _, _, lanes = tp_grid()
    place = lax.axis_index("tp") // lanes

    def part(k):
        return lax.dynamic_index_in_dim(parts, (place + k) % ring, 0, keepdims=False)

    total = part(0).astype(F32)
    if ring != 4:
        for k in range(1, ring):
            total = total + ring_shift(part(k), k).astype(F32)
        return total
    half = parts.shape[2] // 2
    far = part(2)
    from_left, from_right = ring_shift(far[:, :half], 1), ring_shift(far[:, half:], -1)
    ahead, behind = part(1), part(3)
    low = (ahead[:, :half].astype(F32) + from_left.astype(F32)).astype(BF)
    high = (behind[:, half:].astype(F32) + from_right.astype(F32)).astype(BF)
    ahead = jnp.concatenate([low, ahead[:, half:]], 1)
    behind = jnp.concatenate([behind[:, :half], high], 1)
    return total + ring_shift(ahead, 1).astype(F32) + ring_shift(behind, -1).astype(F32)


def reduce_scatter_tp(parts):
    count, ring, lanes = tp_grid()
    lane = lax.axis_index("tp") % lanes
    grid = parts.reshape((ring, lanes) + parts.shape[1:])
    total = None
    for k in list(range(1, lanes)) + [0]:
        picked = lax.dynamic_index_in_dim(grid, (lane + k) % lanes, 1, keepdims=False)
        summed = ring_reduce(picked)
        if k:
            summed = lane_shift(summed.astype(BF), k).astype(F32)
        total = summed if total is None else total + summed
    return total


def spread_rows(own, frames, sub, f_own, rows):
    count, ring, lanes = tp_grid()
    me = lax.axis_index("tp")
    place, lane = me // lanes, me % lanes
    out = jnp.zeros((count,) + own.shape, own.dtype)
    for k in range(lanes):
        column = lane_shift(own, k) if k else own
        for back, piece in ring_pieces(column):
            at = ((place - back) % ring) * lanes + (lane - k) % lanes
            out = lax.dynamic_update_slice(out, piece[None], (at, 0, 0))
    return out.reshape(frames, rows, own.shape[1])


def exchange(parts, axis):
    count = parts.shape[0]
    me = lax.axis_index(axis)
    out = parts
    for k in range(1, count):
        piece = lax.dynamic_index_in_dim(parts, (me + k) % count, 0)
        got = lax.ppermute(piece, axis, [(i, (i + k) % count) for i in range(count)])
        out = lax.dynamic_update_slice_in_dim(out, got, (me - k) % count, 0)
    return out


def solution(mesh):
    placed = (
        P(None, "sp", None),
        P(),
        P("sp", None, "tp"),
        P("tp", "sp"),
        P("sp", "tp"),
        P("tp", "sp"),
    )
    return jax.shard_map(
        shards, mesh=mesh, in_specs=placed, out_specs=P(None, "sp", "tp"), check_vma=False
    )
```

profile of v0, /device:TPU:27, one launch (start us, length us, event | category | flops | bytes accessed | tf_op | source)
XLA Modules:
  0.0 521.1 jit_solution(2116081824539977933)
XLA Ops:
  0.0 5.9 %copy.91 = bf16[8,55,4096]{2,1,0:T(8,128)(2,1)} copy(bf16[8,55,4096]{2,0,1:T(8,128)(2,1)} %param.6) | data formatting | bytes 7208960 | tf_op args[0]
  34.9 11.3 %collective-permute-done.6 = bf16[224,1024]{1,0:T(8,128)(2,1)S(1)} collective-permute-done((bf16[224,1024]{1,0:T(8,128)(2,1)S(1)}, bf16[224,1024]{1,0:T(8,128)(2,1)S(1)}, u32[]{:S(2)}, u32[]{:S(2)}) %collective-permute-start.6) | collective-permute-done | bytes 458784 | tf_op jit(solution)/shard_map/ppermute | solution.py:171
  52.6 5.6 %collective-permute-done.9 = bf16[224,512]{1,0:T(8,128)(2,1)S(1)} collective-permute-done((bf16[224,512]{1,0:T(8,128)(2,1)S(1)}, bf16[224,512]{1,0:T(8,128)(2,1)S(1)}, u32[]{:S(2)}, u32[]{:S(2)}) %collective-permute-start.9) | collective-permute-done | bytes 229408 | tf_op jit(solution)/shard_map/ppermute | solution.py:171
  58.3 9.8 %collective-permute-done.11 = bf16[224,1024]{1,0:T(8,128)(2,1)S(1)} collective-permute-done((bf16[224,1024]{1,0:T(8,128)(2,1)S(1)}, bf16[224,1024]{1,0:T(8,128)(2,1)S(1)}, u32[]{:S(2)}, u32[]{:S(2)}) %collective-permute-start.11) | collective-permute-done | bytes 458784 | tf_op jit(solution)/shard_map/ppermute | solution.py:171
  69.8 8.0 %collective-permute-done.12 = bf16[224,1024]{1,0:T(8,128)(2,1)S(1)} collective-permute-done((bf16[224,1024]{1,0:T(8,128)(2,1)S(1)}, bf16[224,1024]{1,0:T(8,128)(2,1)S(1)}, u32[]{:S(2)}, u32[]{:S(2)}) %collective-permute-start.12) | collective-permute-done | bytes 458784 | tf_op jit(solution)/shard_map/ppermute | solution.py:171
  108.7 12.6 %collective-permute-done.16 = bf16[224,1536]{1,0:T(8,128)(2,1)S(1)} collective-permute-done((bf16[224,1536]{1,0:T(8,128)(2,1)S(1)}, bf16[224,1536]{1,0:T(8,128)(2,1)S(1)}, u32[]{:S(2)}, u32[]{:S(2)}) %collective-permute-start.16) | collective-permute-done | bytes 688160 | tf_op jit(solution)/shard_map/ppermute | solution.py:37
  144.6 6.0 %collective-permute-done.23 = bf16[224,512]{1,0:T(8,128)(2,1)S(1)} collective-permute-done((bf16[224,512]{1,0:T(8,128)(2,1)S(1)}, bf16[224,512]{1,0:T(8,128)(2,1)S(1)}, u32[]{:S(2)}, u32[]{:S(2)}) %collective-permute-start.23) | collective-permute-done | bytes 229408 | tf_op jit(solution)/shard_map/ppermute | solution.py:52
  181.3 7.1 %collective-permute-done.26 = bf16[224,1024]{1,0:T(8,128)(2,1)S(1)} collective-permute-done((bf16[224,1024]{1,0:T(8,128)(2,1)S(1)}, bf16[224,1024]{1,0:T(8,128)(2,1)S(1)}, u32[]{:S(2)}, u32[]{:S(2)}) %collective-permute-start.26) | collective-permute-done | bytes 458784 | tf_op jit(solution)/shard_map/ppermute | solution.py:171
  188.4 10.5 %collective-permute-done.28 = bf16[224,1024]{1,0:T(8,128)(2,1)S(1)} collective-permute-done((bf16[224,1024]{1,0:T(8,128)(2,1)S(1)}, bf16[224,1024]{1,0:T(8,128)(2,1)S(1)}, u32[]{:S(2)}, u32[]{:S(2)}) %collective-permute-start.28) | collective-permute-done | bytes 458784 | tf_op jit(solution)/shard_map/ppermute | solution.py:171
  208.1 10.4 %collective-permute-done.33 = bf16[224,1024]{1,0:T(8,128)(2,1)S(1)} collective-permute-done((bf16[224,1024]{1,0:T(8,128)(2,1)}, bf16[224,1024]{1,0:T(8,128)(2,1)S(1)}, u32[]{:S(2)}, u32[]{:S(2)}) %collective-permute-start.33) | collective-permute-done | bytes 458784 | tf_op jit(solution)/shard_map/ppermute | solution.py:171
  220.4 5.9 %all-gather.1 = f32[4,2,224]{2,1,0:T(2,128)S(1)} all-gather(f32[1,2,224]{2,1,0:T(2,128)S(1)} %maximum_bitcast_fusion.4), channel_id=2, replica_groups=mesh['sp'=4,'tp'=8] {'sp'}, dimensions={0}, use_global_device_ids=true | all-gather | bytes 8960 | tf_op jit(solution)/shard_map/all_gather | solution.py:133
  230.2 8.9 %collective-permute-done.34 = bf16[224,1024]{1,0:T(8,128)(2,1)S(1)} collective-permute-done((bf16[224,1024]{1,0:T(8,128)(2,1)S(1)}, bf16[224,1024]{1,0:T(8,128)(2,1)S(1)}, u32[]{:S(2)}, u32[]{:S(2)}) %collective-permute-start.34) | collective-permute-done | bytes 458784 | tf_op jit(solution)/shard_map/ppermute | solution.py:171
  242.5 6.9 %collective-permute-done.35 = bf16[224,1024]{1,0:T(8,128)(2,1)S(1)} collective-permute-done((bf16[224,1024]{1,0:T(8,128)(2,1)S(1)}, bf16[224,1024]{1,0:T(8,128)(2,1)S(1)}, u32[]{:S(2)}, u32[]{:S(2)}) %collective-permute-start.35) | collective-permute-done | bytes 458784 | tf_op jit(solution)/shard_map/ppermute | solution.py:171
  253.2 5.7 %collective-permute-done.37 = bf16[224,512]{1,0:T(8,128)(2,1)S(1)} collective-permute-done((bf16[224,512]{1,0:T(8,128)(2,1)S(1)}, bf16[224,512]{1,0:T(8,128)(2,1)S(1)}, u32[]{:S(2)}, u32[]{:S(2)}) %collective-permute-start.37) | collective-permute-done | bytes 229408 | tf_op jit(solution)/shard_map/ppermute | solution.py:171
  259.0 9.7 %collective-permute-done.39 = bf16[224,1024]{1,0:T(8,128)(2,1)S(1)} collective-permute-done((bf16[224,1024]{1,0:T(8,128)(2,1)S(1)}, bf16[224,1024]{1,0:T(8,128)(2,1)S(1)}, u32[]{:S(2)}, u32[]{:S(2)}) %collective-permute-start.39) | collective-permute-done | bytes 458784 | tf_op jit(solution)/shard_map/ppermute | solution.py:171
  272.0 6.6 %collective-permute-done.40 = bf16[224,1024]{1,0:T(8,128)(2,1)S(1)} collective-permute-done((bf16[224,1024]{1,0:T(8,128)(2,1)S(1)}, bf16[224,1024]{1,0:T(8,128)(2,1)S(1)}, u32[]{:S(2)}, u32[]{:S(2)}) %collective-permute-start.40) | collective-permute-done | bytes 458784 | tf_op jit(solution)/shard_map/ppermute | solution.py:171
  278.6 10.2 %collective-permute-start.42 = (bf16[224,512]{1,0:T(8,128)(2,1)S(1)}, bf16[224,512]{1,0:T(8,128)(2,1)S(1)}, u32[]{:S(2)}, u32[]{:S(2)}) collective-permute-start(bf16[224,512]{1,0:T(8,128)(2,1)S(1)} %slice.264), channel_id=1, source_target_pairs={{0,6},{1,7},{2,0},{3,1},{4,2},{5,3},{6,4},{7,5},{8,14},{9,15},{10,... | collective-permute-start | bytes 688136 | tf_op jit(solution)/shard_map/ppermute | solution.py:171
  288.9 6.1 %collective-permute-done.42 = bf16[224,512]{1,0:T(8,128)(2,1)S(1)} collective-permute-done((bf16[224,512]{1,0:T(8,128)(2,1)S(1)}, bf16[224,512]{1,0:T(8,128)(2,1)S(1)}, u32[]{:S(2)}, u32[]{:S(2)}) %collective-permute-start.42) | collective-permute-done | bytes 229408 | tf_op jit(solution)/shard_map/ppermute | solution.py:171
  314.1 7.5 %collective-permute-done.59 = bf16[448,512]{1,0:T(8,128)(2,1)S(1)} collective-permute-done((bf16[448,512]{1,0:T(8,128)(2,1)S(1)}, bf16[448,512]{1,0:T(8,128)(2,1)S(1)}, u32[]{:S(2)}, u32[]{:S(2)}) %collective-permute-start.59) | collective-permute-done | bytes 458784 | tf_op jit(solution)/shard_map/ppermute | solution.py:37
  324.5 6.9 %collective-permute-done.49 = bf16[448,512]{1,0:T(8,128)(2,1)S(1)} collective-permute-done((bf16[448,512]{1,0:T(8,128)(2,1)S(1)}, bf16[448,512]{1,0:T(8,128)(2,1)S(1)}, u32[]{:S(2)}, u32[]{:S(2)}) %collective-permute-start.49) | collective-permute-done | bytes 458784 | tf_op jit(solution)/shard_map/ppermute | solution.py:37
  334.3 6.9 %collective-permute-done.44 = bf16[448,512]{1,0:T(8,128)(2,1)S(1)} collective-permute-done((bf16[448,512]{1,0:T(8,128)(2,1)S(1)}, bf16[448,512]{1,0:T(8,128)(2,1)S(1)}, u32[]{:S(2)}, u32[]{:S(2)}) %collective-permute-start.44) | collective-permute-done | bytes 458784 | tf_op jit(solution)/shard_map/ppermute | solution.py:37
  342.1 9.0 %collective-permute-done.54 = bf16[448,512]{1,0:T(8,128)(2,1)S(1)} collective-permute-done((bf16[448,512]{1,0:T(8,128)(2,1)S(1)}, bf16[448,512]{1,0:T(8,128)(2,1)S(1)}, u32[]{:S(2)}, u32[]{:S(2)}) %collective-permute-start.54) | collective-permute-done | bytes 458784 | tf_op jit(solution)/shard_map/ppermute | solution.py:37
  354.2 6.7 %collective-permute-done.61 = bf16[448,512]{1,0:T(8,128)(2,1)S(1)} collective-permute-done((bf16[448,512]{1,0:T(8,128)(2,1)S(1)}, bf16[448,512]{1,0:T(8,128)(2,1)S(1)}, u32[]{:S(2)}, u32[]{:S(2)}) %collective-permute-start.61) | collective-permute-done | bytes 458784 | tf_op jit(solution)/shard_map/ppermute | solution.py:52
  363.4 7.4 %collective-permute-done.51 = bf16[448,512]{1,0:T(8,128)(2,1)S(1)} collective-permute-done((bf16[448,512]{1,0:T(8,128)(2,1)S(1)}, bf16[448,512]{1,0:T(8,128)(2,1)S(1)}, u32[]{:S(2)}, u32[]{:S(2)}) %collective-permute-start.51) | collective-permute-done | bytes 458784 | tf_op jit(solution)/shard_map/ppermute | solution.py:52
  373.1 7.4 %collective-permute-done.46 = bf16[448,512]{1,0:T(8,128)(2,1)S(1)} collective-permute-done((bf16[448,512]{1,0:T(8,128)(2,1)S(1)}, bf16[448,512]{1,0:T(8,128)(2,1)S(1)}, u32[]{:S(2)}, u32[]{:S(2)}) %collective-permute-start.46) | collective-permute-done | bytes 458784 | tf_op jit(solution)/shard_map/ppermute | solution.py:52
  382.8 7.5 %collective-permute-done.56 = bf16[448,512]{1,0:T(8,128)(2,1)S(1)} collective-permute-done((bf16[448,512]{1,0:T(8,128)(2,1)S(1)}, bf16[448,512]{1,0:T(8,128)(2,1)S(1)}, u32[]{:S(2)}, u32[]{:S(2)}) %collective-permute-start.56) | collective-permute-done | bytes 458784 | tf_op jit(solution)/shard_map/ppermute | solution.py:52
  404.3 8.0 %add_convert_fusion = bf16[1792,1024]{1,0:T(8,128)(2,1)S(1)} fusion(f32[1792,1024]{1,0:T(8,128)} %fusion.25, f32[1792,1024]{1,0:T(8,128)} %fusion.31, f32[1792,1024]{1,0:T(8,128)S(1)} %fusion.28, bf16[1792,512]{1,0:T(8,128)(2,1)S(1)} %bitcast.373, bf16[2048,1024]{1,0:T(8,128)(2,1)S(1)} %copy-done.10), kind=kOutput, calls=%fused_computation.2 | convolution fusion | flops 1886388224 | bytes 28573696 | tf_op jit(solution)/shard_map/dot_general | solution.py:148
  416.4 8.5 %collective-permute-done.63 = bf16[224,512]{1,0:T(8,128)(2,1)S(1)} collective-permute-done((bf16[224,512]{1,0:T(8,128)(2,1)S(1)}, bf16[224,512]{1,0:T(8,128)(2,1)S(1)}, u32[]{:S(2)}, u32[]{:S(2)}) %collective-permute-start.63) | collective-permute-done | bytes 229408 | tf_op jit(solution)/shard_map/ppermute | solution.py:171
  426.7 8.0 %collective-permute-done.68 = bf16[224,512]{1,0:T(8,128)(2,1)S(1)} collective-permute-done((bf16[224,512]{1,0:T(8,128)(2,1)S(1)}, bf16[224,512]{1,0:T(8,128)(2,1)S(1)}, u32[]{:S(2)}, u32[]{:S(2)}) %collective-permute-start.68) | collective-permute-done | bytes 229408 | tf_op jit(solution)/shard_map/ppermute | solution.py:171
  436.5 17.8 %collective-permute-done.64 = bf16[224,1024]{1,0:T(8,128)(2,1)S(1)} collective-permute-done((bf16[224,1024]{1,0:T(8,128)(2,1)S(1)}, bf16[224,1024]{1,0:T(8,128)(2,1)S(1)}, u32[]{:S(2)}, u32[]{:S(2)}) %collective-permute-start.64) | collective-permute-done | bytes 458784 | tf_op jit(solution)/shard_map/ppermute | solution.py:171
  455.1 18.9 %collective-permute-done.69 = bf16[224,1024]{1,0:T(8,128)(2,1)S(1)} collective-permute-done((bf16[224,1024]{1,0:T(8,128)(2,1)S(1)}, bf16[224,1024]{1,0:T(8,128)(2,1)S(1)}, u32[]{:S(2)}, u32[]{:S(2)}) %collective-permute-start.69) | collective-permute-done | bytes 458784 | tf_op jit(solution)/shard_map/ppermute | solution.py:171
  500.2 6.8 %collective-permute-done.77 = bf16[1,56,512]{2,0,1:T(2,128)(2,1)S(1)} collective-permute-done((bf16[1,56,512]{2,0,1:T(2,128)(2,1)S(1)}, bf16[1,56,512]{2,0,1:T(2,128)(2,1)S(1)}, u32[]{:S(2)}, u32[]{:S(2)}) %collective-permute-start.77) | collective-permute-done | bytes 57376 | tf_op jit(solution)/shard_map/ppermute | solution.py:250
  (342 shorter events, 244.4 us)
Async XLA Ops:
  27.0 21.9 %collective-permute-start.7 = (bf16[224,1024]{1,0:T(8,128)(2,1)S(1)}, bf16[224,1024]{1,0:T(8,128)(2,1)S(1)}, u32[]{:S(2)}, u32[]{:S(2)}) collective-permute-start(bf16[224,1024]{1,0:T(8,128)(2,1)S(1)} %bitcast.395), channel_id=1, source_target_pairs={{0,6},{1,7},{2,0},{3,1},{4,2},{5,3},{6,4},{7,5},{8,14},{9,15},{10,... | collective-permute-start | bytes 1376264 | tf_op jit(solution)/shard_map/ppermute | solution.py:171
  28.5 21.0 %collective-permute-start.10 = (bf16[224,1024]{1,0:T(8,128)(2,1)S(1)}, bf16[224,1024]{1,0:T(8,128)(2,1)S(1)}, u32[]{:S(2)}, u32[]{:S(2)}) collective-permute-start(bf16[224,1024]{1,0:T(8,128)(2,1)S(1)} %bitcast.396), channel_id=1, source_target_pairs={{0,1},{1,0},{2,3},{3,2},{4,5},{5,4},{6,7},{7,6},{8,9},{9,8},{10,11... | collective-permute-start | bytes 1376264 | tf_op jit(solution)/shard_map/ppermute | solution.py:178
  52.3 25.6 %collective-permute-start.12 = (bf16[224,1024]{1,0:T(8,128)(2,1)S(1)}, bf16[224,1024]{1,0:T(8,128)(2,1)S(1)}, u32[]{:S(2)}, u32[]{:S(2)}) collective-permute-start(bf16[224,1024]{1,0:T(8,128)(2,1)S(1)} %collective-permute-done.10), channel_id=1, source_target_pairs={{0,6},{1,7},{2,0},{3,1},{4,2},{5,3},{6,4},{7,5},{8,14},{9,15},{10,... | collective-permute-start | bytes 1376264 | tf_op jit(solution)/shard_map/ppermute | solution.py:171
  101.9 101.3 %collective-permute-start = (bf16[1,56,1024]{2,1,0:T(8,128)(2,1)}, bf16[1,56,1024]{2,1,0:T(8,128)(2,1)S(1)}, u32[]{:S(2)}, u32[]{:S(2)}) collective-permute-start(bf16[1,56,1024]{2,1,0:T(8,128)(2,1)} %bitcast.365), channel_id=1, source_target_pairs={{0,8},{8,16},{16,24},{24,0},{1,9},{9,17},{17,25},{25,1},{2,10},{10... | collective-permute-start | bytes 344072 | tf_op jit(solution)/shard_map/ppermute | solution.py:250
  108.4 27.8 %collective-permute-start.21 = (bf16[224,1536]{1,0:T(8,128)(2,1)}, bf16[224,1536]{1,0:T(8,128)(2,1)}, u32[]{:S(2)}, u32[]{:S(2)}) collective-permute-start(bf16[224,1536]{1,0:T(8,128)(2,1)} %dynamic-slice_bitcast_fusion.6), channel_id=1, source_target_pairs={{0,16},{8,24},{16,0},{24,8},{1,17},{9,25},{17,1},{25,9},{2,18},{10... | collective-permute-start | bytes 2064392 | tf_op jit(solution)/shard_map/ppermute | solution.py:37
  131.1 20.5 %collective-permute-start.17 = (bf16[224,512]{1,0:T(8,128)(2,1)}, bf16[224,512]{1,0:T(8,128)(2,1)}, u32[]{:S(2)}, u32[]{:S(2)}) collective-permute-start(bf16[224,512]{1,0:T(8,128)(2,1)} %bitcast.362), channel_id=1, source_target_pairs={{0,8},{8,0},{16,24},{24,16},{1,9},{9,1},{17,25},{25,17},{2,10},{10... | collective-permute-start | bytes 688136 | tf_op jit(solution)/shard_map/ppermute | solution.py:53
  164.0 24.4 %collective-permute-start.26 = (bf16[224,1024]{1,0:T(8,128)(2,1)S(1)}, bf16[224,1024]{1,0:T(8,128)(2,1)S(1)}, u32[]{:S(2)}, u32[]{:S(2)}) collective-permute-start(bf16[224,1024]{1,0:T(8,128)(2,1)S(1)} %pad_maximum_fusion.1), channel_id=1, source_target_pairs={{0,2},{1,3},{2,4},{3,5},{4,6},{5,7},{6,0},{7,1},{8,10},{9,11},{10,... | collective-permute-start | bytes 1376264 | tf_op jit(solution)/shard_map/ppermute | solution.py:171
  169.4 29.4 %collective-permute-start.28 = (bf16[224,1024]{1,0:T(8,128)(2,1)S(1)}, bf16[224,1024]{1,0:T(8,128)(2,1)S(1)}, u32[]{:S(2)}, u32[]{:S(2)}) collective-permute-start(bf16[224,1024]{1,0:T(8,128)(2,1)S(1)} %pad_maximum_fusion.2), channel_id=1, source_target_pairs={{0,6},{1,7},{2,0},{3,1},{4,2},{5,3},{6,4},{7,5},{8,14},{9,15},{10,... | collective-permute-start | bytes 1376264 | tf_op jit(solution)/shard_map/ppermute | solution.py:171
  174.6 33.5 %collective-permute-start.31 = (bf16[224,1024]{1,0:T(8,128)(2,1)}, bf16[224,1024]{1,0:T(8,128)(2,1)S(1)}, u32[]{:S(2)}, u32[]{:S(2)}) collective-permute-start(bf16[224,1024]{1,0:T(8,128)(2,1)} %pad_maximum_fusion.3), channel_id=1, source_target_pairs={{0,2},{1,3},{2,4},{3,5},{4,6},{5,7},{6,0},{7,1},{8,10},{9,11},{10,... | collective-permute-start | bytes 1376264 | tf_op jit(solution)/shard_map/ppermute | solution.py:171
  180.1 38.5 %collective-permute-start.33 = (bf16[224,1024]{1,0:T(8,128)(2,1)}, bf16[224,1024]{1,0:T(8,128)(2,1)S(1)}, u32[]{:S(2)}, u32[]{:S(2)}) collective-permute-start(bf16[224,1024]{1,0:T(8,128)(2,1)} %pad_maximum_fusion.4), channel_id=1, source_target_pairs={{0,6},{1,7},{2,0},{3,1},{4,2},{5,3},{6,4},{7,5},{8,14},{9,15},{10,... | collective-permute-start | bytes 1376264 | tf_op jit(solution)/shard_map/ppermute | solution.py:171
  228.7 20.7 %collective-permute-start.35 = (bf16[224,1024]{1,0:T(8,128)(2,1)S(1)}, bf16[224,1024]{1,0:T(8,128)(2,1)S(1)}, u32[]{:S(2)}, u32[]{:S(2)}) collective-permute-start(bf16[224,1024]{1,0:T(8,128)(2,1)S(1)} %get-tuple-element.16), channel_id=1, source_target_pairs={{0,6},{1,7},{2,0},{3,1},{4,2},{5,3},{6,4},{7,5},{8,14},{9,15},{10,... | collective-permute-start | bytes 1376264 | tf_op jit(solution)/shard_map/ppermute | solution.py:171
  228.7 21.8 %collective-permute-start.38 = (bf16[224,1024]{1,0:T(8,128)(2,1)S(1)}, bf16[224,1024]{1,0:T(8,128)(2,1)S(1)}, u32[]{:S(2)}, u32[]{:S(2)}) collective-permute-start(bf16[224,1024]{1,0:T(8,128)(2,1)S(1)} %get-tuple-element.16), channel_id=1, source_target_pairs={{0,1},{1,0},{2,3},{3,2},{4,5},{5,4},{6,7},{7,6},{8,9},{9,8},{10,11... | collective-permute-start | bytes 1376264 | tf_op jit(solution)/shard_map/ppermute | solution.py:178
  252.7 25.9 %collective-permute-start.40 = (bf16[224,1024]{1,0:T(8,128)(2,1)S(1)}, bf16[224,1024]{1,0:T(8,128)(2,1)S(1)}, u32[]{:S(2)}, u32[]{:S(2)}) collective-permute-start(bf16[224,1024]{1,0:T(8,128)(2,1)S(1)} %collective-permute-done.38), channel_id=1, source_target_pairs={{0,6},{1,7},{2,0},{3,1},{4,2},{5,3},{6,4},{7,5},{8,14},{9,15},{10,... | collective-permute-start | bytes 1376264 | tf_op jit(solution)/shard_map/ppermute | solution.py:171
  310.3 21.1 %collective-permute-start.49 = (bf16[448,512]{1,0:T(8,128)(2,1)S(1)}, bf16[448,512]{1,0:T(8,128)(2,1)S(1)}, u32[]{:S(2)}, u32[]{:S(2)}) collective-permute-start(bf16[448,512]{1,0:T(8,128)(2,1)S(1)} %dynamic-slice_bitcast_fusion.16), channel_id=1, source_target_pairs={{0,16},{8,24},{16,0},{24,8},{1,17},{9,25},{17,1},{25,9},{2,18},{10... | collective-permute-start | bytes 1376264 | tf_op jit(solution)/shard_map/ppermute | solution.py:37
  312.1 29.1 %collective-permute-start.44 = (bf16[448,512]{1,0:T(8,128)(2,1)S(1)}, bf16[448,512]{1,0:T(8,128)(2,1)S(1)}, u32[]{:S(2)}, u32[]{:S(2)}) collective-permute-start(bf16[448,512]{1,0:T(8,128)(2,1)S(1)} %dynamic-slice_bitcast_fusion.17), channel_id=1, source_target_pairs={{0,16},{8,24},{16,0},{24,8},{1,17},{9,25},{17,1},{25,9},{2,18},{10... | collective-permute-start | bytes 1376264 | tf_op jit(solution)/shard_map/ppermute | solution.py:37
  312.9 38.2 %collective-permute-start.54 = (bf16[448,512]{1,0:T(8,128)(2,1)S(1)}, bf16[448,512]{1,0:T(8,128)(2,1)S(1)}, u32[]{:S(2)}, u32[]{:S(2)}) collective-permute-start(bf16[448,512]{1,0:T(8,128)(2,1)S(1)} %dynamic-slice_bitcast_fusion.15), channel_id=1, source_target_pairs={{0,16},{8,24},{16,0},{24,8},{1,17},{9,25},{17,1},{25,9},{2,18},{10... | collective-permute-start | bytes 1376264 | tf_op jit(solution)/shard_map/ppermute | solution.py:37
  322.1 32.0 %collective-permute-start.60 = (bf16[448,512]{1,0:T(8,128)(2,1)S(1)}, bf16[448,512]{1,0:T(8,128)(2,1)S(1)}, u32[]{:S(2)}, u32[]{:S(2)}) collective-permute-start(bf16[448,512]{1,0:T(8,128)(2,1)S(1)} %get-tuple-element.8), channel_id=1, source_target_pairs={{0,8},{8,0},{16,24},{24,16},{1,9},{9,1},{17,25},{25,17},{2,10},{10... | collective-permute-start | bytes 1376264 | tf_op jit(solution)/shard_map/ppermute | solution.py:53
  324.5 36.4 %collective-permute-start.61 = (bf16[448,512]{1,0:T(8,128)(2,1)S(1)}, bf16[448,512]{1,0:T(8,128)(2,1)S(1)}, u32[]{:S(2)}, u32[]{:S(2)}) collective-permute-start(bf16[448,512]{1,0:T(8,128)(2,1)S(1)} %get-tuple-element.8), channel_id=1, source_target_pairs={{0,16},{8,24},{16,0},{24,8},{1,17},{9,25},{17,1},{25,9},{2,18},{10... | collective-permute-start | bytes 1376264 | tf_op jit(solution)/shard_map/ppermute | solution.py:52
  331.9 31.3 %collective-permute-start.50 = (bf16[448,512]{1,0:T(8,128)(2,1)S(1)}, bf16[448,512]{1,0:T(8,128)(2,1)S(1)}, u32[]{:S(2)}, u32[]{:S(2)}) collective-permute-start(bf16[448,512]{1,0:T(8,128)(2,1)S(1)} %get-tuple-element.10), channel_id=1, source_target_pairs={{0,8},{8,0},{16,24},{24,16},{1,9},{9,1},{17,25},{25,17},{2,10},{10... | collective-permute-start | bytes 1376264 | tf_op jit(solution)/shard_map/ppermute | solution.py:53
  341.2 29.5 %collective-permute-start.51 = (bf16[448,512]{1,0:T(8,128)(2,1)S(1)}, bf16[448,512]{1,0:T(8,128)(2,1)S(1)}, u32[]{:S(2)}, u32[]{:S(2)}) collective-permute-start(bf16[448,512]{1,0:T(8,128)(2,1)S(1)} %get-tuple-element.10), channel_id=1, source_target_pairs={{0,16},{8,24},{16,0},{24,8},{1,17},{9,25},{17,1},{25,9},{2,18},{10... | collective-permute-start | bytes 1376264 | tf_op jit(solution)/shard_map/ppermute | solution.py:52
  351.1 22.0 %collective-permute-start.45 = (bf16[448,512]{1,0:T(8,128)(2,1)S(1)}, bf16[448,512]{1,0:T(8,128)(2,1)S(1)}, u32[]{:S(2)}, u32[]{:S(2)}) collective-permute-start(bf16[448,512]{1,0:T(8,128)(2,1)S(1)} %get-tuple-element.12), channel_id=1, source_target_pairs={{0,8},{8,0},{16,24},{24,16},{1,9},{9,1},{17,25},{25,17},{2,10},{10... | collective-permute-start | bytes 1376264 | tf_op jit(solution)/shard_map/ppermute | solution.py:53
  354.1 26.4 %collective-permute-start.46 = (bf16[448,512]{1,0:T(8,128)(2,1)S(1)}, bf16[448,512]{1,0:T(8,128)(2,1)S(1)}, u32[]{:S(2)}, u32[]{:S(2)}) collective-permute-start(bf16[448,512]{1,0:T(8,128)(2,1)S(1)} %get-tuple-element.12), channel_id=1, source_target_pairs={{0,16},{8,24},{16,0},{24,8},{1,17},{9,25},{17,1},{25,9},{2,18},{10... | collective-permute-start | bytes 1376264 | tf_op jit(solution)/shard_map/ppermute | solution.py:52
  360.9 30.9 %collective-permute-start.55 = (bf16[448,512]{1,0:T(8,128)(2,1)S(1)}, bf16[448,512]{1,0:T(8,128)(2,1)S(1)}, u32[]{:S(2)}, u32[]{:S(2)}) collective-permute-start(bf16[448,512]{1,0:T(8,128)(2,1)S(1)} %get-tuple-element.14), channel_id=1, source_target_pairs={{0,8},{8,0},{16,24},{24,16},{1,9},{9,1},{17,25},{25,17},{2,10},{10... | collective-permute-start | bytes 1376264 | tf_op jit(solution)/shard_map/ppermute | solution.py:53
  363.2 27.2 %collective-permute-start.56 = (bf16[448,512]{1,0:T(8,128)(2,1)S(1)}, bf16[448,512]{1,0:T(8,128)(2,1)S(1)}, u32[]{:S(2)}, u32[]{:S(2)}) collective-permute-start(bf16[448,512]{1,0:T(8,128)(2,1)S(1)} %get-tuple-element.14), channel_id=1, source_target_pairs={{0,16},{8,24},{16,0},{24,8},{1,17},{9,25},{17,1},{25,9},{2,18},{10... | collective-permute-start | bytes 1376264 | tf_op jit(solution)/shard_map/ppermute | solution.py:52
  370.7 33.5 %collective-permute-start.62 = (bf16[448,512]{1,0:T(8,128)(2,1)S(1)}, bf16[448,512]{1,0:T(8,128)(2,1)S(1)}, u32[]{:S(2)}, u32[]{:S(2)}) collective-permute-start(bf16[448,512]{1,0:T(8,128)(2,1)S(1)} %collective-permute-done.61), channel_id=1, source_target_pairs={{0,8},{8,0},{16,24},{24,16},{1,9},{9,1},{17,25},{25,17},{2,10},{10... | collective-permute-start | bytes 1376264 | tf_op jit(solution)/shard_map/ppermute | solution.py:53
  425.0 29.4 %collective-permute-start.64 = (bf16[224,1024]{1,0:T(8,128)(2,1)S(1)}, bf16[224,1024]{1,0:T(8,128)(2,1)S(1)}, u32[]{:S(2)}, u32[]{:S(2)}) collective-permute-start(bf16[224,1024]{1,0:T(8,128)(2,1)S(1)} %pad_maximum_fusion.5), channel_id=1, source_target_pairs={{0,2},{1,3},{2,4},{3,5},{4,6},{5,7},{6,0},{7,1},{8,10},{9,11},{10,... | collective-permute-start | bytes 1376264 | tf_op jit(solution)/shard_map/ppermute | solution.py:171
  425.2 29.2 %collective-permute-start.66 = (bf16[224,1024]{1,0:T(8,128)(2,1)S(1)}, bf16[224,1024]{1,0:T(8,128)(2,1)S(1)}, u32[]{:S(2)}, u32[]{:S(2)}) collective-permute-start(bf16[224,1024]{1,0:T(8,128)(2,1)S(1)} %pad_maximum_fusion.6), channel_id=1, source_target_pairs={{0,6},{1,7},{2,0},{3,1},{4,2},{5,3},{6,4},{7,5},{8,14},{9,15},{10,... | collective-permute-start | bytes 1376264 | tf_op jit(solution)/shard_map/ppermute | solution.py:171
  434.8 39.2 %collective-permute-start.69 = (bf16[224,1024]{1,0:T(8,128)(2,1)S(1)}, bf16[224,1024]{1,0:T(8,128)(2,1)S(1)}, u32[]{:S(2)}, u32[]{:S(2)}) collective-permute-start(bf16[224,1024]{1,0:T(8,128)(2,1)S(1)} %pad_maximum_fusion.7), channel_id=1, source_target_pairs={{0,2},{1,3},{2,4},{3,5},{4,6},{5,7},{6,0},{7,1},{8,10},{9,11},{10,... | collective-permute-start | bytes 1376264 | tf_op jit(solution)/shard_map/ppermute | solution.py:171
  435.0 39.0 %collective-permute-start.71 = (bf16[224,1024]{1,0:T(8,128)(2,1)S(1)}, bf16[224,1024]{1,0:T(8,128)(2,1)S(1)}, u32[]{:S(2)}, u32[]{:S(2)}) collective-permute-start(bf16[224,1024]{1,0:T(8,128)(2,1)S(1)} %pad_maximum_fusion.8), channel_id=1, source_target_pairs={{0,6},{1,7},{2,0},{3,1},{4,2},{5,3},{6,4},{7,5},{8,14},{9,15},{10,... | collective-permute-start | bytes 1376264 | tf_op jit(solution)/shard_map/ppermute | solution.py:171
  490.3 21.9 %collective-permute-start.79 = (bf16[1,56,512]{2,0,1:T(2,128)(2,1)S(1)}, bf16[1,56,512]{2,0,1:T(2,128)(2,1)S(1)}, u32[]{:S(2)}, u32[]{:S(2)}) collective-permute-start(bf16[1,56,512]{2,0,1:T(2,128)(2,1)S(1)} %get-tuple-element.35), channel_id=1, source_target_pairs={{0,5},{1,6},{2,7},{3,0},{4,1},{5,2},{6,3},{7,4},{8,13},{9,14},{10,... | collective-permute-start | bytes 172040 | tf_op jit(solution)/shard_map/ppermute | solution.py:250
  492.4 22.3 %collective-permute-start.80 = (bf16[1,56,512]{2,0,1:T(2,128)(2,1)S(1)}, bf16[1,56,512]{2,0,1:T(2,128)(2,1)S(1)}, u32[]{:S(2)}, u32[]{:S(2)}) collective-permute-start(bf16[1,56,512]{2,0,1:T(2,128)(2,1)S(1)} %get-tuple-element.34), channel_id=1, source_target_pairs={{0,6},{1,7},{2,0},{3,1},{4,2},{5,3},{6,4},{7,5},{8,14},{9,15},{10,... | collective-permute-start | bytes 172040 | tf_op jit(solution)/shard_map/ppermute | solution.py:250
  493.3 24.0 %collective-permute-start.81 = (bf16[1,56,512]{2,0,1:T(2,128)(2,1)S(1)}, bf16[1,56,512]{2,0,1:T(2,128)(2,1)S(1)}, u32[]{:S(2)}, u32[]{:S(2)}) collective-permute-start(bf16[1,56,512]{2,0,1:T(2,128)(2,1)S(1)} %get-tuple-element.33), channel_id=1, source_target_pairs={{0,7},{1,0},{2,1},{3,2},{4,3},{5,4},{6,5},{7,6},{8,15},{9,8},{10,9... | collective-permute-start | bytes 172040 | tf_op jit(solution)/shard_map/ppermute | solution.py:250
  (62 other events, 944.9 us)
where the time goes:
time: 530 us; the launch traced here: 521 us
  waiting for transfers between devices  283 us (53%)
  starting transfers between devices  110 us (21%)
  local copies, waits for them, and re-layouts  58.1 us (11%)
  matrix products  42 us (8%)
  other arithmetic  19.9 us (4%)
  blocking collectives  5.89 us (1%)
    ppermute x32, waiting for transfers between devices, ring_shift(): lax.ppermute(value, 'tp', [(i, (i // lanes + k) % ring * lanes + i % lane...  177 us
    ppermute x32, starting transfers between devices, ring_shift(): lax.ppermute(value, 'tp', [(i, (i // lanes + k) % ring * lanes + i % lane...  50.1 us
    ppermute x6, waiting for transfers between devices, reduce_scatter_sp(): total = total + lax.ppermute(piece, 'sp', perm).astype(F32)  46.2 us
    ppermute x6, waiting for transfers between devices, all_gather_sp(): got = lax.ppermute(piece, 'sp', perm)  35 us
    ppermute x16, waiting for transfers between devices, exchange(): lax.ppermute(piece, axis, [(i, (i + k) % count) for i in range(count)])  25.2 us
    dynamic_update_slice x16, local copies, waits for them, and re-layouts, exchange(): out = lax.dynamic_update_slice_in_dim(out, got, (me - k) % count, 0)  22.5 us
    ppermute x12, starting transfers between devices, all_gather_sp(): other = lax.ppermute(got, 'sp', [(i, i ^ 1) for i in range(sp_count)])  20.9 us
    dot_general x4, matrix products, shards(): jnp.dot(hidden, w_down[c * hid:(c + 1) * hid], preferred_element_type=F32)  20.2 us
  transfers between devices with their start and end apart: 82, of which 46 were waited for; matrix products, arithmetic and copies ran while one was open for 15% of the time, Pallas kernels for 0%

commit v1 on v0

--- a/solution.py
+++ b/solution.py
@@ -3,6 +3,8 @@
 import jax
 import jax.numpy as jnp
 from jax import lax
+from jax.experimental import pallas as pl
+from jax.experimental.pallas import tpu as pltpu
 from jax.sharding import PartitionSpec as P
 
 DH = 128
@@ -103,7 +105,8 @@
     h_split = sp_count // f_split
     f_mine, h_mine = f_chunk // f_split, heads // h_split
     w_flat = w_qkv.reshape(slab, 3 * heads * DH)
-    attn_parts = []
+    attn_parts, att_all = [], []
+    fused = tail_fits(frames, rows, heads, w_up.shape[1])
     for c in range(chunks):
         lhs = mod_a[c * f_chunk : (c + 1) * f_chunk].reshape(f_chunk * rows, slab)
         proj = jnp.dot(lhs, w_flat, preferred_element_type=F32).astype(BF)
@@ -120,7 +123,15 @@
             att = att.reshape(f_split, h_split, f_mine * rows, h_mine * DH)
             att = jnp.transpose(att, (0, 2, 1, 3))
         att = att.reshape(f_chunk * rows, heads * DH)
+        att_all.append(att)
+        if fused:
+            continue
         attn_parts.append(jnp.dot(att, w_out, preferred_element_type=F32).astype(BF))
+    if fused:
+        att = jnp.concatenate(att_all, 0)
+        mod_slice = lax.dynamic_slice_in_dim(modulation, sp_me * slab, slab, 1)
+        block = run_tail(att, tok_slab, mod_slice, w_out, w_up, w_down, frames, part)
+        return block[:, :patches]
     attn_part = jnp.concatenate(attn_parts, 0).reshape(tp_count, own_rows, slab)
     attn_sum = reduce_scatter_tp(attn_part)
 
@@ -158,6 +169,448 @@
     block = block.reshape(groups, sub, f_own, part, width // tp_count)
     block = jnp.transpose(block, (0, 2, 1, 3, 4)).reshape(frames, padded, width // tp_count)
     return block[:, :patches]
+
+
+def tail_fits(frames, rows, heads, hidden):
+    sp_count, tp_count = lax.axis_size("sp"), lax.axis_size("tp")
+    _, ring, lanes = tp_grid()
+    return (
+        sp_count == 4
+        and lanes == 2
+        and ring > 1
+        and tp_count == frames
+        and rows % 32 == 0
+        and rows <= 256
+        and (heads * DH) % 256 == 0
+        and hidden % 1024 == 0
+    )
+
+
+def tile_loop(count, body):
+    def step(i, carry):
+        body(i)
+        return carry
+
+    lax.fori_loop(0, count, step, 0)
+
+
+def tail_kernel(
+    att_ref, tok_ref, mod_ref, w_out_ref, w_up_ref, w_down_ref, out_ref,
+    wo, wu, wd, part, partm, y_in, z_in, modb, up_out, up_in, up_own, hid, acc, mid, fin, st,
+    w_sem, wx_send, wx_recv, y_send, y_recv, z_send, z_recv, st_send, st_recv,
+    az_send, az_recv, ay_send, ay_recv, ap_send, ap_recv, u_send, u_recv,
+    hx_send, hx_recv, hp_send, hp_recv, hf_send, hf_recv, o_send, o_recv,
+):
+    sp, tp = lax.axis_index("sp"), lax.axis_index("tp")
+    count, ring, lanes = tp_grid()
+    core, chip = lax.rem(sp, 2), lax.div(sp, 2)
+    z, y = lax.div(tp, lanes), lax.rem(tp, lanes)
+    lane = 1 - y
+    partner, across = chip * 2 + (1 - core), (1 - chip) * 2 + core
+    total, rows, inner = att_ref.shape
+    slab = wo.shape[1]
+    half, quarter = wu.shape[1], up_out.shape[2]
+    width = 4 * slab
+    parts, part_rows = fin.shape[0], fin.shape[1]
+    lanes_wide = out_ref.shape[2]
+    per_slab = slab // lanes_wide
+    group = rows // 2
+
+    def rc(src, dst, ssem, rsem, **dev):
+        return pltpu.make_async_remote_copy(
+            src_ref=src, dst_ref=dst, send_sem=ssem, recv_sem=rsem,
+            device_id=dev, device_id_type=pl.DeviceIdType.MESH,
+        )
+
+    def near(k):
+        low = z < ring // 2
+        zz = jnp.where(low, z, ring - 1 - z)
+        at = jnp.where(k == 0, zz, jnp.where(k <= zz, k - 1, k))
+        return jnp.where(low, at, ring - 1 - at)
+
+    local = [
+        pltpu.make_async_copy(w_out_ref, wo, w_sem.at[0]),
+        pltpu.make_async_copy(
+            w_up_ref.at[:, pl.ds(pl.multiple_of(core * half, 128), half)],
+            wu.at[pl.ds(pl.multiple_of(core * slab, 128), slab)],
+            w_sem.at[1],
+        ),
+        pltpu.make_async_copy(w_down_ref, wd, w_sem.at[2]),
+    ]
+    for c in local:
+        c.start()
+    swap = rc(
+        w_up_ref.at[:, pl.ds(pl.multiple_of((1 - core) * half, 128), half)],
+        wu.at[pl.ds(pl.multiple_of(core * slab, 128), slab)],
+        wx_send, wx_recv, sp=partner,
+    )
+    swap.start()
+    local[0].wait()
+
+    def y_copy(p, buf, zf):
+        return rc(buf.at[zf * lanes + lane], y_in.at[p, zf], y_send.at[p, zf], y_recv.at[p, zf], tp=z * lanes + lane)
+
+    def z_copy(p, buf, zf):
+        up = zf > z
+        nxt = jnp.where(up, z + 1, z - 1)
+        slot = jnp.where(jnp.logical_and(nxt == zf, z > zf), ring, zf)
+        return rc(buf.at[zf * lanes + y], z_in.at[p, slot], z_send.at[p, zf], z_recv.at[p, slot], tp=nxt * lanes + y)
+
+    def add_rows(dst, src):
+        def body(i):
+            at = pl.ds(pl.multiple_of(i * 32, 32), 32)
+            dst[at, :] = dst[at, :] + src[at, :].astype(F32)
+        tile_loop(rows // 32, body)
+
+    def gather_sum(p, buf, zf):
+        y_copy(p, buf, zf).wait_recv()
+        f = zf * lanes + y
+
+        def body(i):
+            at = pl.ds(pl.multiple_of(i * 32, 32), 32)
+            acc[at, :] = buf[f, at, :].astype(F32) + y_in[p, zf, at, :].astype(F32)
+        tile_loop(rows // 32, body)
+
+        def take(slot):
+            pltpu.make_async_copy(z_in.at[p, slot], z_in.at[p, slot], z_recv.at[p, slot]).wait()
+            add_rows(acc, z_in.at[p, slot])
+
+        @pl.when(jnp.logical_and(zf >= z, z > 0))
+        def _():
+            take(zf)
+
+        @pl.when(jnp.logical_and(zf <= z, z < ring - 1))
+        def _():
+            take(jnp.where(zf == z, ring, zf))
+
+    def reduce_tp(p, buf):
+        def step(k):
+            zf = near(ring - 1 - k)
+            gather_sum(p, buf, zf)
+            f = zf * lanes + y
+
+            @pl.when(zf != z)
+            def _():
+                def body(i):
+                    at = pl.ds(pl.multiple_of(i * 32, 32), 32)
+                    buf[f, at, :] = acc[at, :].astype(BF)
+                tile_loop(rows // 32, body)
+                z_copy(p, buf, zf).start()
+        tile_loop(ring, step)
+
+    def reduce_done(p, buf):
+        def step(zf):
+            y_copy(p, buf, zf).wait_send()
+
+            @pl.when(zf != z)
+            def _():
+                z_copy(p, buf, zf).wait_send()
+        tile_loop(ring, step)
+
+    def project(k):
+        zf = near(ring - 1 - k)
+        for d in (lane, y):
+            f = zf * lanes + d
+
+            def body(n):
+                cols = pl.ds(pl.multiple_of(n * 256, 256), 256)
+                part[f, :, cols] = jnp.dot(att_ref[f], wo[:, cols], preferred_element_type=F32).astype(BF)
+            tile_loop(slab // 256, body)
+            if d is lane:
+                y_copy(0, part, zf).start()
+    tile_loop(ring, project)
+    reduce_tp(0, part)
+
+    eye = lax.broadcasted_iota(jnp.int32, (group, 128), 0) == lax.broadcasted_iota(jnp.int32, (group, 128), 1)
+
+    def to_row(col):
+        return jnp.sum(jnp.where(eye, col, 0.0), axis=0, keepdims=True)
+
+    def to_col(row):
+        return jnp.sum(jnp.where(eye, jnp.broadcast_to(row, (group, 128)), 0.0), axis=1, keepdims=True)
+
+    for g in range(2):
+        at = pl.ds(g * group, group)
+        value = (tok_ref[at, :].astype(F32) + mod_ref[2:3, :] * acc[at, :]).astype(BF).astype(F32)
+        mid[at, :] = value
+        mean_s = jnp.sum(value, axis=1, keepdims=True) / slab
+        dev_s = jnp.sum(jnp.square(value - mean_s), axis=1, keepdims=True)
+        st[sp, pl.ds(g, 1), :] = to_row(mean_s)
+        st[sp, pl.ds(2 + g, 1), :] = to_row(dev_s)
+    def st_copy(k):
+        return rc(st.at[sp], st.at[sp], st_send.at[k - 1], st_recv.at[k - 1], sp=lax.rem(sp + k, 4))
+    for k in range(1, 4):
+        st_copy(k).start()
+    for k in range(1, 4):
+        got = lax.rem(sp + 4 - k, 4)
+        rc(st.at[got], st.at[got], st_send.at[k - 1], st_recv.at[k - 1], sp=got).wait_recv()
+    for g in range(2):
+        at = pl.ds(g * group, group)
+        means = [st[s, pl.ds(g, 1), :] for s in range(4)]
+        devs = [st[s, pl.ds(2 + g, 1), :] for s in range(4)]
+        center = (means[0] + means[1] + means[2] + means[3]) / 4
+        spread = devs[0] + devs[1] + devs[2] + devs[3]
+        for m in means:
+            spread = spread + slab * jnp.square(m - center)
+        scale = to_col(lax.rsqrt(spread / width + EPSILON))
+        value = (mid[at, :] - to_col(center)) * scale
+        modb[core, tp, at, :] = (value * (1.0 + mod_ref[4:5, :]) + mod_ref[3:4, :]).astype(BF)
+
+    def az_copy(zs, up):
+        f = zs * lanes + y
+        nxt = jnp.where(up, z + 1, z - 1)
+        side = jnp.where(up, 1, 0)
+        return rc(modb.at[core, f], modb.at[core, f], az_send.at[side, zs], az_recv.at[zs], tp=nxt * lanes + y)
+
+    def ay_copy(zs, at_y):
+        f = zs * lanes + at_y
+        return rc(modb.at[core, f], modb.at[core, f], ay_send.at[zs], ay_recv.at[zs], tp=z * lanes + lane)
+
+    def ap_copy(slab_at, f):
+        return rc(modb.at[slab_at, f], modb.at[slab_at, f], ap_send.at[f], ap_recv.at[f], sp=partner)
+
+    def serve(k):
+        zs = near(k)
+
+        @pl.when(zs != z)
+        def _():
+            az_copy(zs, True).wait_recv()
+
+        @pl.when(jnp.logical_and(zs <= z, z < ring - 1))
+        def _():
+            az_copy(zs, True).start()
+
+        @pl.when(jnp.logical_and(zs >= z, z > 0))
+        def _():
+            az_copy(zs, False).start()
+        ay_copy(zs, y).start()
+        ap_copy(core, zs * lanes + y).start()
+
+    def serve_lane(k):
+        zs = near(k)
+        ay_copy(zs, lane).wait_recv()
+        ap_copy(core, zs * lanes + lane).start()
+
+    serve(0)
+    local[1].wait()
+    swap.wait()
+    local[2].wait()
+
+    def piece(i):
+        zs = near(lax.div(i, lanes))
+        d = lax.rem(i, lanes)
+        return zs, jnp.where(d == 0, y, lane)
+
+    def u_copy(f):
+        return rc(up_out.at[f], up_in.at[f], u_send.at[f], u_recv.at[f], sp=across)
+
+    def cols_of(who_chip, who_core):
+        return pl.ds(pl.multiple_of(who_core * half + who_chip * quarter, 128), quarter)
+
+    def hx_copy(f, who):
+        ref = hid.at[f, :, cols_of(who, core)]
+        return rc(ref, ref, hx_send.at[f], hx_recv.at[f], sp=across)
+
+    def hp_copy(f, who):
+        ref = hid.at[f, :, cols_of(chip, who)]
+        return rc(ref, ref, hp_send.at[f], hp_recv.at[f], sp=partner)
+
+    def hf_copy(f, who):
+        ref = hid.at[f, :, cols_of(1 - chip, who)]
+        return rc(ref, ref, hf_send.at[f], hf_recv.at[f], sp=partner)
+
+    def stage_up(i):
+        zs, at_y = piece(i)
+        f = zs * lanes + at_y
+        ap_copy(1 - core, f).wait_recv()
+
+        def product(col):
+            cols = pl.ds(pl.multiple_of(col, 128), 256)
+            return jnp.dot(modb[0, f], wu[0:slab, cols], preferred_element_type=F32) + jnp.dot(
+                modb[1, f], wu[slab : 2 * slab, cols], preferred_element_type=F32
+            )
+
+        def away(n):
+            up_out[f, :, pl.ds(pl.multiple_of(n * 256, 256), 256)] = product((1 - chip) * quarter + n * 256).astype(BF)
+        tile_loop(quarter // 256, away)
+        u_copy(f).start()
+
+        def home(n):
+            up_own[lax.rem(i, 2), :, pl.ds(pl.multiple_of(n * 256, 256), 256)] = product(chip * quarter + n * 256)
+        tile_loop(quarter // 256, home)
+
+    def stage_gelu(i):
+        zs, at_y = piece(i)
+        f = zs * lanes + at_y
+        u_copy(f).wait_recv()
+
+        def body(j):
+            at = pl.ds(pl.multiple_of(j * 32, 32), 32)
+            v = up_own[lax.rem(i, 2), at, :] + up_in[f, at, :].astype(F32)
+            hid[f, at, cols_of(chip, core)] = jax.nn.gelu(v, approximate=True).astype(BF)
+        tile_loop(rows // 32, body)
+        hx_copy(f, chip).start()
+        hp_copy(f, core).start()
+
+    def stage_forward(i):
+        zs, at_y = piece(i)
+        f = zs * lanes + at_y
+        hx_copy(f, 1 - chip).wait_recv()
+        hf_copy(f, core).start()
+
+    def stage_down(i):
+        zs, at_y = piece(i)
+        f = zs * lanes + at_y
+        hp_copy(f, 1 - core).wait_recv()
+        hf_copy(f, 1 - core).wait_recv()
+
+        def body(n):
+            cols = pl.ds(pl.multiple_of(n * 256, 256), 256)
+            partm[f, :, cols] = jnp.dot(hid[f], wd[:, cols], preferred_element_type=F32).astype(BF)
+        tile_loop(slab // 256, body)
+
+        @pl.when(at_y == lane)
+        def _():
+            y_copy(1, partm, zs).start()
+
+    def mlp(i):
+        @pl.when(i < total)
+        def _():
+            stage_up(i)
+
+        @pl.when(jnp.logical_and(i >= 1, i < total + 1))
+        def _():
+            stage_gelu(i - 1)
+
+        @pl.when(jnp.logical_and(i >= 2, i < total + 2))
+        def _():
+            stage_forward(i - 2)
+
+        @pl.when(i >= 3)
+        def _():
+            stage_down(i - 3)
+
+        @pl.when(i + 1 < ring)
+        def _():
+            serve(i + 1)
+
+        @pl.when(jnp.logical_and(i + 1 < total, lax.rem(i + 1, lanes) != 0))
+        def _():
+            serve_lane(lax.div(i + 1, lanes))
+    tile_loop(total + 3, mlp)
+    reduce_tp(1, partm)
+
+    for j in range(parts):
+        at = pl.ds(j * part_rows, part_rows)
+        fin[j] = (mid[at, :] + mod_ref[5:6, :] * acc[at, :]).astype(BF)
+
+    def o_copy(j, q):
+        at = tp * parts + j
+        frame, to_sp, to_tp = lax.div(at, 4), lax.rem(at, 4), sp * per_slab + q
+        src = fin.at[j, :, pl.ds(q * lanes_wide, lanes_wide)]
+        here = jnp.logical_and(to_sp == sp, to_tp == tp)
+        far = rc(src, out_ref.at[frame], o_send.at[j * per_slab + q], o_recv.at[frame], sp=to_sp, tp=to_tp)
+        near_by = pltpu.make_async_copy(src, out_ref.at[frame], o_recv.at[frame])
+        return here, far, near_by
+
+    for j in range(parts):
+        for q in range(per_slab):
+            here, far, near_by = o_copy(j, q)
+
+            @pl.when(here)
+            def _():
+                near_by.start()
+
+            @pl.when(jnp.logical_not(here))
+            def _():
+                far.start()
+
+    for k in range(1, 4):
+        st_copy(k).wait_send()
+    reduce_done(0, part)
+    reduce_done(1, partm)
+
+    def drain(zs):
+        @pl.when(jnp.logical_and(zs <= z, z < ring - 1))
+        def _():
+            az_copy(zs, True).wait_send()
+
+        @pl.when(jnp.logical_and(zs >= z, z > 0))
+        def _():
+            az_copy(zs, False).wait_send()
+        ay_copy(zs, y).wait_send()
+    tile_loop(ring, drain)
+
+    def drain_pieces(f):
+        ap_copy(core, f).wait_send()
+        u_copy(f).wait_send()
+        hx_copy(f, chip).wait_send()
+        hp_copy(f, core).wait_send()
+        hf_copy(f, core).wait_send()
+    tile_loop(total, drain_pieces)
+    for j in range(parts):
+        for q in range(per_slab):
+            here, far, _ = o_copy(j, q)
+
+            @pl.when(jnp.logical_not(here))
+            def _():
+                far.wait_send()
+    for frame in range(out_ref.shape[0]):
+        pltpu.make_async_copy(out_ref.at[frame], out_ref.at[frame], o_recv.at[frame]).wait()
+
+
+def run_tail(att, tok_slab, mod_slice, w_out, w_up, w_down, frames, part):
+    sp_count, tp_count = lax.axis_size("sp"), lax.axis_size("tp")
+    _, ring, lanes = tp_grid()
+    total = tp_count
+    rows, slab = tok_slab.shape
+    inner, hidden = w_out.shape[0], w_up.shape[1]
+    half, quarter = hidden // 2, hidden // 4
+    parts = rows // part
+    wide = sp_count * slab // tp_count
+    dma = pltpu.SemaphoreType.DMA
+    vm = pl.BlockSpec(memory_space=pltpu.VMEM)
+    hbm = pl.BlockSpec(memory_space=pl.ANY)
+    flops = 2 * total * rows * slab * (inner + 2 * hidden)
+    return pl.pallas_call(
+        tail_kernel,
+        name="tail",
+        out_shape=jax.ShapeDtypeStruct((frames, part, wide), BF),
+        in_specs=[vm, vm, vm, hbm, hbm, hbm],
+        out_specs=hbm,
+        scratch_shapes=[
+            pltpu.VMEM((inner, slab), BF),
+            pltpu.VMEM((2 * slab, half), BF),
+            pltpu.VMEM((hidden, slab), BF),
+            pltpu.VMEM((total, rows, slab), BF),
+            pltpu.VMEM((total, rows, slab), BF),
+            pltpu.VMEM((2, ring, rows, slab), BF),
+            pltpu.VMEM((2, ring + 1, rows, slab), BF),
+            pltpu.VMEM((2, total, rows, slab), BF),
+            pltpu.VMEM((total, rows, quarter), BF),
+            pltpu.VMEM((total, rows, quarter), BF),
+            pltpu.VMEM((2, rows, quarter), F32),
+            pltpu.VMEM((total, rows, hidden), BF),
+            pltpu.VMEM((rows, slab), F32),
+            pltpu.VMEM((rows, slab), F32),
+            pltpu.VMEM((parts, part, slab), BF),
+            pltpu.VMEM((4, 8, 128), F32),
+            dma((3,)), dma, dma,
+            dma((2, ring)), dma((2, ring)),
+            dma((2, ring)), dma((2, ring + 1)),
+            dma((3,)), dma((3,)),
+            dma((2, ring)), dma((ring,)),
+            dma((ring,)), dma((ring,)),
+            dma((total,)), dma((total,)),
+            dma((total,)), dma((total,)),
+            dma((total,)), dma((total,)),
+            dma((total,)), dma((total,)),
+            dma((total,)), dma((total,)),
+            dma((parts * (slab // wide),)), dma((frames,)),
+        ],
+        compiler_params=pltpu.CompilerParams(has_side_effects=True, vmem_limit_bytes=64000000),
+        cost_estimate=pl.CostEstimate(flops=flops, bytes_accessed=2 * rows * slab * total, transcendentals=0),
+    )(att.reshape(total, rows, inner), tok_slab, mod_slice, w_out, w_up, w_down)
 
 
 def tp_grid():

time: 530 us -> 394 us (0.74)
  the two profiles are of different devices: /device:TPU:27 before, /device:TPU:3 now
where the time goes in v1:
time: 394 us
  Pallas kernels  227 us (58%)
  waiting for transfers between devices  93.1 us (24%)
  local copies, waits for them, and re-layouts  33.5 us (9%)
  starting transfers between devices  23.7 us (6%)
  matrix products  8.82 us (2%)
  other arithmetic  7.28 us (2%)
    pallas_call x1, Pallas kernels, run_tail(): pl.pallas_call(tail_kernel, name='tail', out_shape=jax.ShapeDtypeStruct((...  227 us
    ppermute x8, waiting for transfers between devices, ring_shift(): lax.ppermute(value, 'tp', [(i, (i // lanes + k) % ring * lanes + i % lane...  43.4 us
    ppermute x2, waiting for transfers between devices, reduce_scatter_sp(): total = total + lax.ppermute(piece, 'sp', perm).astype(F32)  27.2 us
    ppermute x6, waiting for transfers between devices, exchange(): lax.ppermute(piece, axis, [(i, (i + k) % count) for i in range(count)])  16.1 us
    unnamed x14, local copies, waits for them, and re-layouts  12.7 us
    dynamic_update_slice x8, local copies, waits for them, and re-layouts, exchange(): out = lax.dynamic_update_slice_in_dim(out, got, (me - k) % count, 0)  10.1 us
    ppermute x8, starting transfers between devices, ring_shift(): lax.ppermute(value, 'tp', [(i, (i // lanes + k) % ring * lanes + i % lane...  9.11 us
  transfers between devices with their start and end apart: 25, of which 15 were waited for; matrix products, arithmetic and copies ran while one was open for 7% of the time, Pallas kernels for 0%

profile of v1, /device:TPU:3, one launch (start us, length us, event | category | flops | bytes accessed | tf_op | source)
XLA Modules:
  0.0 394.0 jit_solution(5047523046689779030)
XLA Ops:
  0.0 5.8 %copy.25 = bf16[8,55,4096]{2,1,0:T(8,128)(2,1)} copy(bf16[8,55,4096]{2,0,1:T(8,128)(2,1)} %param.6) | data formatting | bytes 7208960 | tf_op args[0]
  8.8 2.0 collective-permute-start.1
  10.8 2.5 collective-permute-done
  13.2 1.5 dynamic_update_slice.66
  14.7 6.2 %collective-permute-done.1 = bf16[1,56,1024]{2,0,1:T(2,128)(2,1)S(1)} collective-permute-done((bf16[1,56,1024]{2,0,1:T(2,128)(2,1)S(1)}, bf16[1,56,1024]{2,0,1:T(2,128)(2,1)S(1)}, u32[]{:S(2)}, u32[]{:S(2)}) %collective-permute-start.1) | collective-permute-done | bytes 114720 | tf_op jit(solution)/shard_map/ppermute | solution.py:703
  20.9 1.5 dynamic_update_slice.67
  22.4 1.5 dynamic_update_slice.68
  25.4 2.1 collective-permute-start.4
  28.8 4.6 %copy.28 = bf16[1024,3,512]{0,2,1:T(8,128)(2,1)} copy(bf16[1024,3,512]{2,0,1:T(8,128)(2,1)} %param.8) | data formatting | bytes 6291456 | tf_op args[2]
  33.9 4.4 %collective-permute-done.3 = bf16[224,1024]{1,0:T(8,128)(2,1)S(1)} collective-permute-done((bf16[224,1024]{1,0:T(8,128)(2,1)S(1)}, bf16[224,1024]{1,0:T(8,128)(2,1)S(1)}, u32[]{:S(2)}, u32[]{:S(2)}) %collective-permute-start.3) | collective-permute-done | bytes 458784 | tf_op jit(solution)/shard_map/ppermute | solution.py:624
  38.4 9.8 %collective-permute-done.4 = bf16[224,1024]{1,0:T(8,128)(2,1)S(1)} collective-permute-done((bf16[224,1024]{1,0:T(8,128)(2,1)S(1)}, bf16[224,1024]{1,0:T(8,128)(2,1)S(1)}, u32[]{:S(2)}, u32[]{:S(2)}) %collective-permute-start.4) | collective-permute-done | bytes 458784 | tf_op jit(solution)/shard_map/ppermute | solution.py:624
  49.8 2.9 collective-permute-start.9
  52.8 12.3 %collective-permute-done.6 = bf16[224,512]{1,0:T(8,128)(2,1)S(1)} collective-permute-done((bf16[224,512]{1,0:T(8,128)(2,1)S(1)}, bf16[224,512]{1,0:T(8,128)(2,1)S(1)}, u32[]{:S(2)}, u32[]{:S(2)}) %collective-permute-start.6) | collective-permute-done | bytes 229408 | tf_op jit(solution)/shard_map/ppermute | solution.py:624
  65.3 1.8 collective-permute-done.8
  67.2 10.1 %collective-permute-done.9 = bf16[224,1024]{1,0:T(8,128)(2,1)S(1)} collective-permute-done((bf16[224,1024]{1,0:T(8,128)(2,1)S(1)}, bf16[224,1024]{1,0:T(8,128)(2,1)S(1)}, u32[]{:S(2)}, u32[]{:S(2)}) %collective-permute-start.9) | collective-permute-done | bytes 458784 | tf_op jit(solution)/shard_map/ppermute | solution.py:624
  78.5 2.3 collective-permute-done.10
  80.7 2.7 collective-permute-done.11
  83.9 1.5 copy-done
  85.4 3.3 convolution_convert_fusion.1
  90.1 4.6 %collective-permute-start.12 = (bf16[2,224,1536]{2,1,0:T(8,128)(2,1)}, bf16[2,224,1536]{2,1,0:T(8,128)(2,1)}, u32[]{:S(2)}, u32[]{:S(2)}) collective-permute-start(bf16[2,224,1536]{2,1,0:T(8,128)(2,1)} %dynamic-slice_bitcast_fusion.1), channel_id=1, source_target_pairs={{0,8},{8,0},{16,24},{24,16},{1,9},{9,1},{17,25},{25,17},{2,10},{10... | collective-permute-start | bytes 4128776 | tf_op jit(solution)/shard_map/ppermute | solution.py:32
  94.6 3.3 convolution_convert_fusion
  103.9 2.5 collective-permute-done.22
  106.4 1.5 dynamic_update_slice.85
  107.9 5.0 %collective-permute-done.23 = bf16[1,56,1024]{2,0,1:T(2,128)(2,1)S(1)} collective-permute-done((bf16[1,56,1024]{2,0,1:T(2,128)(2,1)S(1)}, bf16[1,56,1024]{2,0,1:T(2,128)(2,1)S(1)}, u32[]{:S(2)}, u32[]{:S(2)}) %collective-permute-start.23) | collective-permute-done | bytes 114720 | tf_op jit(solution)/shard_map/ppermute | solution.py:703
  112.9 1.5 dynamic_update_slice.86
  114.4 1.5 dynamic_update_slice.87
  116.9 2.2 fusion.3
  122.0 14.8 %collective-permute-done.13 = bf16[224,1536]{1,0:T(8,128)(2,1)S(1)} collective-permute-done((bf16[224,1536]{1,0:T(8,128)(2,1)S(1)}, bf16[224,1536]{1,0:T(8,128)(2,1)S(1)}, u32[]{:S(2)}, u32[]{:S(2)}) %collective-permute-start.13) | collective-permute-done | bytes 688160 | tf_op jit(solution)/shard_map/ppermute | solution.py:39
  139.1 12.3 %collective-permute-done.18 = bf16[224,1536]{1,0:T(8,128)(2,1)} collective-permute-done((bf16[224,1536]{1,0:T(8,128)(2,1)}, bf16[224,1536]{1,0:T(8,128)(2,1)}, u32[]{:S(2)}, u32[]{:S(2)}) %collective-permute-start.18) | collective-permute-done | bytes 688160 | tf_op jit(solution)/shard_map/ppermute | solution.py:39
  155.8 5.4 %collective-permute-done.20 = bf16[224,512]{1,0:T(8,128)(2,1)S(1)} collective-permute-done((bf16[224,512]{1,0:T(8,128)(2,1)S(1)}, bf16[224,512]{1,0:T(8,128)(2,1)S(1)}, u32[]{:S(2)}, u32[]{:S(2)}) %collective-permute-start.20) | collective-permute-done | bytes 229408 | tf_op jit(solution)/shard_map/ppermute | solution.py:54
  165.0 227.1 %tail.1 = bf16[8,56,512]{2,1,0:T(8,128)(2,1)} custom-call(bf16[8,224,512]{2,1,0:T(8,128)(2,1)} %bitcast.184, bf16[224,1024]{1,0:T(8,128)(2,1)} %bitcast.193, f32[6,1024]{1,0:T(8,128)} %constant_dynamic-slice_fusion.mod_ref, bf16[512,1024]{1,0:T(8,128)(2,1)} %w_out_ref.1, bf16[1024,2048]{1,0:T(8,128)(2,1)} %w_up_ref.1, bf16[2048,1024]{1,0:T(8,128)(2,1)} %w_down_ref.1), custom_call_target="tpu_custom_call" | custom-call | flops 16911433728 | bytes 3670016 | tf_op jit(solution)/shard_map/tail/pallas_call | solution.py:575
  392.1 1.9 copy.40
  (101 shorter events, 30.9 us)
Async XLA Ops:
  5.8 1.5 copy-start.4
  8.7 4.5 %collective-permute-start = (bf16[1,56,1024]{2,0,1:T(2,128)(2,1)S(1)}, bf16[1,56,1024]{2,0,1:T(2,128)(2,1)S(1)}, u32[]{:S(2)}, u32[]{:S(2)}) collective-permute-start(bf16[1,56,1024]{2,0,1:T(2,128)(2,1)S(1)} %get-tuple-element.14), channel_id=1, source_target_pairs={{0,8},{8,16},{16,24},{24,0},{1,9},{9,17},{17,25},{25,1},{2,10},{10... | collective-permute-start | bytes 344072 | tf_op jit(solution)/shard_map/ppermute | solution.py:703
  8.8 12.1 %collective-permute-start.1 = (bf16[1,56,1024]{2,0,1:T(2,128)(2,1)S(1)}, bf16[1,56,1024]{2,0,1:T(2,128)(2,1)S(1)}, u32[]{:S(2)}, u32[]{:S(2)}) collective-permute-start(bf16[1,56,1024]{2,0,1:T(2,128)(2,1)S(1)} %get-tuple-element.13), channel_id=1, source_target_pairs={{0,16},{8,24},{16,0},{24,8},{1,17},{9,25},{17,1},{25,9},{2,18},{10... | collective-permute-start | bytes 344072 | tf_op jit(solution)/shard_map/ppermute | solution.py:703
  10.8 11.6 %collective-permute-start.2 = (bf16[1,56,1024]{2,0,1:T(2,128)(2,1)S(1)}, bf16[1,56,1024]{2,0,1:T(2,128)(2,1)S(1)}, u32[]{:S(2)}, u32[]{:S(2)}) collective-permute-start(bf16[1,56,1024]{2,0,1:T(2,128)(2,1)S(1)} %get-tuple-element.12), channel_id=1, source_target_pairs={{0,24},{8,0},{16,8},{24,16},{1,25},{9,1},{17,9},{25,17},{2,26},{10... | collective-permute-start | bytes 344072 | tf_op jit(solution)/shard_map/ppermute | solution.py:703
  24.1 14.2 %collective-permute-start.3 = (bf16[224,1024]{1,0:T(8,128)(2,1)S(1)}, bf16[224,1024]{1,0:T(8,128)(2,1)S(1)}, u32[]{:S(2)}, u32[]{:S(2)}) collective-permute-start(bf16[224,1024]{1,0:T(8,128)(2,1)S(1)} %bitcast.185), channel_id=1, source_target_pairs={{0,2},{1,3},{2,4},{3,5},{4,6},{5,7},{6,0},{7,1},{8,10},{9,11},{10,... | collective-permute-start | bytes 1376264 | tf_op jit(solution)/shard_map/ppermute | solution.py:624
  25.4 22.8 %collective-permute-start.4 = (bf16[224,1024]{1,0:T(8,128)(2,1)S(1)}, bf16[224,1024]{1,0:T(8,128)(2,1)S(1)}, u32[]{:S(2)}, u32[]{:S(2)}) collective-permute-start(bf16[224,1024]{1,0:T(8,128)(2,1)S(1)} %bitcast.186), channel_id=1, source_target_pairs={{0,6},{1,7},{2,0},{3,1},{4,2},{5,3},{6,4},{7,5},{8,14},{9,15},{10,... | collective-permute-start | bytes 1376264 | tf_op jit(solution)/shard_map/ppermute | solution.py:624
  27.5 21.9 %collective-permute-start.7 = (bf16[224,1024]{1,0:T(8,128)(2,1)S(1)}, bf16[224,1024]{1,0:T(8,128)(2,1)S(1)}, u32[]{:S(2)}, u32[]{:S(2)}) collective-permute-start(bf16[224,1024]{1,0:T(8,128)(2,1)S(1)} %bitcast.187), channel_id=1, source_target_pairs={{0,1},{1,0},{2,3},{3,2},{4,5},{5,4},{6,7},{7,6},{8,9},{9,8},{10,11... | collective-permute-start | bytes 1376264 | tf_op jit(solution)/shard_map/ppermute | solution.py:631
  38.3 14.5 %collective-permute-start.5 = (bf16[224,512]{1,0:T(8,128)(2,1)S(1)}, bf16[224,512]{1,0:T(8,128)(2,1)S(1)}, u32[]{:S(2)}, u32[]{:S(2)}) collective-permute-start(bf16[224,512]{1,0:T(8,128)(2,1)S(1)} %slice.66), channel_id=1, source_target_pairs={{0,2},{1,3},{2,4},{3,5},{4,6},{5,7},{6,0},{7,1},{8,10},{9,11},{10,... | collective-permute-start | bytes 688136 | tf_op jit(solution)/shard_map/ppermute | solution.py:624
  48.2 16.9 %collective-permute-start.6 = (bf16[224,512]{1,0:T(8,128)(2,1)S(1)}, bf16[224,512]{1,0:T(8,128)(2,1)S(1)}, u32[]{:S(2)}, u32[]{:S(2)}) collective-permute-start(bf16[224,512]{1,0:T(8,128)(2,1)S(1)} %slice.67), channel_id=1, source_target_pairs={{0,6},{1,7},{2,0},{3,1},{4,2},{5,3},{6,4},{7,5},{8,14},{9,15},{10,... | collective-permute-start | bytes 688136 | tf_op jit(solution)/shard_map/ppermute | solution.py:624
  49.4 17.6 %collective-permute-start.8 = (bf16[224,1024]{1,0:T(8,128)(2,1)S(1)}, bf16[224,1024]{1,0:T(8,128)(2,1)S(1)}, u32[]{:S(2)}, u32[]{:S(2)}) collective-permute-start(bf16[224,1024]{1,0:T(8,128)(2,1)S(1)} %collective-permute-done.7), channel_id=1, source_target_pairs={{0,2},{1,3},{2,4},{3,5},{4,6},{5,7},{6,0},{7,1},{8,10},{9,11},{10,... | collective-permute-start | bytes 1376264 | tf_op jit(solution)/shard_map/ppermute | solution.py:624
  49.8 27.5 %collective-permute-start.9 = (bf16[224,1024]{1,0:T(8,128)(2,1)S(1)}, bf16[224,1024]{1,0:T(8,128)(2,1)S(1)}, u32[]{:S(2)}, u32[]{:S(2)}) collective-permute-start(bf16[224,1024]{1,0:T(8,128)(2,1)S(1)} %collective-permute-done.7), channel_id=1, source_target_pairs={{0,6},{1,7},{2,0},{3,1},{4,2},{5,3},{6,4},{7,5},{8,14},{9,15},{10,... | collective-permute-start | bytes 1376264 | tf_op jit(solution)/shard_map/ppermute | solution.py:624
  67.1 13.7 %collective-permute-start.10 = (bf16[224,512]{1,0:T(8,128)(2,1)S(1)}, bf16[224,512]{1,0:T(8,128)(2,1)S(1)}, u32[]{:S(2)}, u32[]{:S(2)}) collective-permute-start(bf16[224,512]{1,0:T(8,128)(2,1)S(1)} %slice.68), channel_id=1, source_target_pairs={{0,2},{1,3},{2,4},{3,5},{4,6},{5,7},{6,0},{7,1},{8,10},{9,11},{10,... | collective-permute-start | bytes 688136 | tf_op jit(solution)/shard_map/ppermute | solution.py:624
  77.3 6.2 %collective-permute-start.11 = (bf16[224,512]{1,0:T(8,128)(2,1)S(1)}, bf16[224,512]{1,0:T(8,128)(2,1)S(1)}, u32[]{:S(2)}, u32[]{:S(2)}) collective-permute-start(bf16[224,512]{1,0:T(8,128)(2,1)S(1)} %slice.69), channel_id=1, source_target_pairs={{0,6},{1,7},{2,0},{3,1},{4,2},{5,3},{6,4},{7,5},{8,14},{9,15},{10,... | collective-permute-start | bytes 688136 | tf_op jit(solution)/shard_map/ppermute | solution.py:624
  83.5 1.9 copy-start
  88.7 5.9 %copy-start.3 = (bf16[896,1536]{1,0:T(8,128)(2,1)}, bf16[896,1536]{1,0:T(8,128)(2,1)S(1)}, u32[]{:S(2)}) copy-start(bf16[896,1536]{1,0:T(8,128)(2,1)S(1)} %convolution_convert_fusion.1) | copy-start | bytes 8257540
  90.1 26.8 %collective-permute-start.12 = (bf16[2,224,1536]{2,1,0:T(8,128)(2,1)}, bf16[2,224,1536]{2,1,0:T(8,128)(2,1)}, u32[]{:S(2)}, u32[]{:S(2)}) collective-permute-start(bf16[2,224,1536]{2,1,0:T(8,128)(2,1)} %dynamic-slice_bitcast_fusion.1), channel_id=1, source_target_pairs={{0,8},{8,0},{16,24},{24,16},{1,9},{9,1},{17,25},{25,17},{2,10},{10... | collective-permute-start | bytes 4128776 | tf_op jit(solution)/shard_map/ppermute | solution.py:32
  97.9 2.0 copy-start.1
  99.9 19.6 %collective-permute-start.17 = (bf16[2,224,1536]{2,1,0:T(8,128)(2,1)}, bf16[2,224,1536]{2,1,0:T(8,128)(2,1)S(1)}, u32[]{:S(2)}, u32[]{:S(2)}) collective-permute-start(bf16[2,224,1536]{2,1,0:T(8,128)(2,1)} %dynamic-slice_bitcast_fusion), channel_id=1, source_target_pairs={{0,8},{8,0},{16,24},{24,16},{1,9},{9,1},{17,25},{25,17},{2,10},{10... | collective-permute-start | bytes 4128776 | tf_op jit(solution)/shard_map/ppermute | solution.py:32
  101.8 4.6 %collective-permute-start.22 = (bf16[1,56,1024]{2,0,1:T(2,128)(2,1)S(1)}, bf16[1,56,1024]{2,0,1:T(2,128)(2,1)S(1)}, u32[]{:S(2)}, u32[]{:S(2)}) collective-permute-start(bf16[1,56,1024]{2,0,1:T(2,128)(2,1)S(1)} %get-tuple-element.11), channel_id=1, source_target_pairs={{0,8},{8,16},{16,24},{24,0},{1,9},{9,17},{17,25},{25,1},{2,10},{10... | collective-permute-start | bytes 344072 | tf_op jit(solution)/shard_map/ppermute | solution.py:703
  101.8 11.0 %collective-permute-start.23 = (bf16[1,56,1024]{2,0,1:T(2,128)(2,1)S(1)}, bf16[1,56,1024]{2,0,1:T(2,128)(2,1)S(1)}, u32[]{:S(2)}, u32[]{:S(2)}) collective-permute-start(bf16[1,56,1024]{2,0,1:T(2,128)(2,1)S(1)} %get-tuple-element.10), channel_id=1, source_target_pairs={{0,16},{8,24},{16,0},{24,8},{1,17},{9,25},{17,1},{25,9},{2,18},{10... | collective-permute-start | bytes 344072 | tf_op jit(solution)/shard_map/ppermute | solution.py:703
  103.2 11.2 %collective-permute-start.24 = (bf16[1,56,1024]{2,0,1:T(2,128)(2,1)S(1)}, bf16[1,56,1024]{2,0,1:T(2,128)(2,1)S(1)}, u32[]{:S(2)}, u32[]{:S(2)}) collective-permute-start(bf16[1,56,1024]{2,0,1:T(2,128)(2,1)S(1)} %get-tuple-element.9), channel_id=1, source_target_pairs={{0,24},{8,0},{16,8},{24,16},{1,25},{9,1},{17,9},{25,17},{2,26},{10... | collective-permute-start | bytes 344072 | tf_op jit(solution)/shard_map/ppermute | solution.py:703
  116.9 2.7 copy-start.2
  119.2 17.6 %collective-permute-start.13 = (bf16[224,1536]{1,0:T(8,128)(2,1)S(1)}, bf16[224,1536]{1,0:T(8,128)(2,1)S(1)}, u32[]{:S(2)}, u32[]{:S(2)}) collective-permute-start(bf16[224,1536]{1,0:T(8,128)(2,1)S(1)} %dynamic-slice_bitcast_fusion.3), channel_id=1, source_target_pairs={{0,16},{8,24},{16,0},{24,8},{1,17},{9,25},{17,1},{25,9},{2,18},{10... | collective-permute-start | bytes 2064392 | tf_op jit(solution)/shard_map/ppermute | solution.py:39
  120.8 30.6 %collective-permute-start.18 = (bf16[224,1536]{1,0:T(8,128)(2,1)}, bf16[224,1536]{1,0:T(8,128)(2,1)}, u32[]{:S(2)}, u32[]{:S(2)}) collective-permute-start(bf16[224,1536]{1,0:T(8,128)(2,1)} %dynamic-slice_bitcast_fusion.2), channel_id=1, source_target_pairs={{0,16},{8,24},{16,0},{24,8},{1,17},{9,25},{17,1},{25,9},{2,18},{10... | collective-permute-start | bytes 2064392 | tf_op jit(solution)/shard_map/ppermute | solution.py:39
  138.6 23.9 %collective-permute-start.14 = (bf16[224,512]{1,0:T(8,128)(2,1)S(1)}, bf16[224,512]{1,0:T(8,128)(2,1)S(1)}, u32[]{:S(2)}, u32[]{:S(2)}) collective-permute-start(bf16[224,512]{1,0:T(8,128)(2,1)S(1)} %bitcast.195), channel_id=1, source_target_pairs={{0,8},{8,0},{16,24},{24,16},{1,9},{9,1},{17,25},{25,17},{2,10},{10... | collective-permute-start | bytes 688136 | tf_op jit(solution)/shard_map/ppermute | solution.py:55
  138.7 16.3 %collective-permute-start.15 = (bf16[224,512]{1,0:T(8,128)(2,1)S(1)}, bf16[224,512]{1,0:T(8,128)(2,1)S(1)}, u32[]{:S(2)}, u32[]{:S(2)}) collective-permute-start(bf16[224,512]{1,0:T(8,128)(2,1)S(1)} %bitcast.196), channel_id=1, source_target_pairs={{0,16},{8,24},{16,0},{24,8},{1,17},{9,25},{17,1},{25,9},{2,18},{10... | collective-permute-start | bytes 688136 | tf_op jit(solution)/shard_map/ppermute | solution.py:54
  154.3 8.2 %collective-permute-start.19 = (bf16[224,512]{1,0:T(8,128)(2,1)S(1)}, bf16[224,512]{1,0:T(8,128)(2,1)S(1)}, u32[]{:S(2)}, u32[]{:S(2)}) collective-permute-start(bf16[224,512]{1,0:T(8,128)(2,1)S(1)} %bitcast.197), channel_id=1, source_target_pairs={{0,8},{8,0},{16,24},{24,16},{1,9},{9,1},{17,25},{25,17},{2,10},{10... | collective-permute-start | bytes 688136 | tf_op jit(solution)/shard_map/ppermute | solution.py:55
  154.4 6.8 %collective-permute-start.20 = (bf16[224,512]{1,0:T(8,128)(2,1)S(1)}, bf16[224,512]{1,0:T(8,128)(2,1)S(1)}, u32[]{:S(2)}, u32[]{:S(2)}) collective-permute-start(bf16[224,512]{1,0:T(8,128)(2,1)S(1)} %bitcast.198), channel_id=1, source_target_pairs={{0,16},{8,24},{16,0},{24,8},{1,17},{9,25},{17,1},{25,9},{2,18},{10... | collective-permute-start | bytes 688136 | tf_op jit(solution)/shard_map/ppermute | solution.py:54
  155.0 7.6 %collective-permute-start.16 = (bf16[224,512]{1,0:T(8,128)(2,1)S(1)}, bf16[224,512]{1,0:T(8,128)(2,1)S(1)}, u32[]{:S(2)}, u32[]{:S(2)}) collective-permute-start(bf16[224,512]{1,0:T(8,128)(2,1)S(1)} %collective-permute-done.15), channel_id=1, source_target_pairs={{0,8},{8,0},{16,24},{24,16},{1,9},{9,1},{17,25},{25,17},{2,10},{10... | collective-permute-start | bytes 688136 | tf_op jit(solution)/shard_map/ppermute | solution.py:55
  161.2 2.4 collective-permute-start.21
